TPU v7x, 32 devices: a whole 2x2x4 slice. The times are simulated.
32 devices in a mesh: dp: 16 (over z, x, core), tensor: 2 (over y).
Axes of the slice: x: 2, y: 2, z: 4, core: 2. Of those that a mesh axis runs over, the one named last changes fastest.
Arguments:
- x_in: bfloat16 [16, 2, 1024, 768], P(None, 'tensor', 'dp'), may hold values from -6 to 6
- cotangent: bfloat16 [16, 2, 1024, 768], P(None, 'tensor', 'dp'), may hold values from -6 to 6
- lengths: int32 [16], replicated, may hold values from 1 to 2048, 24576 in all
- dealing: int32 [16], replicated, may hold values from 0 to 15, each once
- w_qkv: float32 [768, 3, 768], P('dp', None, 'tensor'), may hold values from -0.21875 to 0.21875
- w_out: float32 [768, 768], P('dp', 'tensor'), may hold values from -1.75 to 1.75
- w_in: float32 [768, 3072], P('dp', 'tensor'), may hold values from -0.21875 to 0.21875
- w_ffo: float32 [768, 3072], P('dp', 'tensor'), may hold values from -0.109375 to 0.109375
- b_qv: float32 [2, 768], P(None, 'tensor'), may hold values from -3 to 3
- b_out: float32 [768], replicated, may hold values from -3 to 3
- b_in: float32 [3072], P('tensor'), may hold values from -3 to 3
- b_ffo: float32 [768], replicated, may hold values from -3 to 3
- ln1_gain: float32 [768], replicated, may hold values from 0.1 to 1.9
- ln1_bias: float32 [768], replicated, may hold values from -3 to 3
- ln2_gain: float32 [768], replicated, may hold values from 0.1 to 1.9
- ln2_bias: float32 [768], replicated, may hold values from -3 to 3
Outputs:
- out: bfloat16 [16, 2, 1024, 768], P(None, 'tensor', 'dp')
- grad_in: bfloat16 [16, 2, 1024, 768], P(None, 'tensor', 'dp')
- grad_w_qkv: float32 [768, 3, 768], P('dp', None, 'tensor')
- grad_w_out: float32 [768, 768], P('dp', 'tensor')
- grad_w_in: float32 [768, 3072], P('dp', 'tensor')
- grad_w_ffo: float32 [768, 3072], P('dp', 'tensor')
- grad_b_qv: float32 [2, 768], P(None, 'tensor')
- grad_b_out: float32 [768], replicated
- grad_b_in: float32 [3072], P('tensor')
- grad_b_ffo: float32 [768], replicated
- grad_ln1_gain: float32 [768], replicated
- grad_ln1_bias: float32 [768], replicated
- grad_ln2_gain: float32 [768], replicated
- grad_ln2_bias: float32 [768], replicated
Inputs may be any that keep to these rules, and one draw needn't show every extreme that they name: Slot j holds lengths[j] tokens of its sequence and padding after them; some slot is full, 2048 tokens. Sequence s goes to slot dealing[s]; every slot gets one sequence.
All inputs are finite; a program needn't handle non-finite values.
Results may differ from a plain program's by a relative error of at most 0.018.
Values may be sent and summed in bfloat16 or wider, within the bound.
A program may use at most 192 MiB of HBM per device.

v0:
```python
import jax
import jax.numpy as jnp
from jax import lax
from jax.sharding import PartitionSpec as P

HEAD_DIM = 64


def slot_owner(dealing):
    places = jnp.arange(dealing.shape[0], dtype=jnp.int32)
    matches = dealing[None, :] == places[:, None]
    return jnp.sum(jnp.where(matches, places[None, :], 0), axis=1)


def contract_last(left_side, right_side):
    return lax.dot_general(
        left_side, right_side, (((1,), (1,)), ((), ())), preferred_element_type=jnp.float32
    )


def contract_first(left_side, right_side):
    return lax.dot_general(
        left_side, right_side, (((0,), (0,)), ((), ())), preferred_element_type=jnp.float32
    )


def norm_forward(values, norm_gain, norm_shift):
    centre = jnp.mean(values, axis=-1, keepdims=True)
    centred = values - centre
    inverse = lax.rsqrt(jnp.mean(centred * centred, axis=-1, keepdims=True) + 1e-06)
    normed = centred * inverse
    return (normed * norm_gain + norm_shift, normed, inverse)


def norm_backward(upstream, normed, inverse, norm_gain):
    scaled = upstream * norm_gain
    back_rows = inverse * (
        scaled
        - jnp.mean(scaled, axis=-1, keepdims=True)
        - normed * jnp.mean(scaled * normed, axis=-1, keepdims=True)
    )
    return (back_rows, jnp.sum(upstream * normed, axis=0), jnp.sum(upstream, axis=0))


def gelu_slope(values):
    return (
        0.5 * (1.0 + lax.erf(values * 0.7071067811865476))
        + values * jnp.exp(-0.5 * values * values) * 0.3989422804014327
    )


def head_forward(query_rows, key_rows, value_rows, key_valid, block_rows, score_scale):
    outputs = []
    totals = []
    for row_start in range(0, query_rows.shape[0], block_rows):
        scores = (
            contract_last(query_rows[row_start : row_start + block_rows], key_rows) * score_scale
        )
        scores = jnp.where(key_valid[None, :], scores, -jnp.inf)
        maxima = jnp.max(scores, axis=1, keepdims=True)
        weights = jnp.exp(scores - maxima)
        summed = jnp.sum(weights, axis=1, keepdims=True)
        probs_low = (weights / summed).astype(jnp.bfloat16)
        outputs.append(jnp.dot(probs_low, value_rows, preferred_element_type=jnp.float32))
        totals.append((maxima + jnp.log(summed))[:, 0])
    return (jnp.concatenate(outputs, axis=0), jnp.concatenate(totals, axis=0))


def head_backward(
    query_rows, key_rows, value_rows, mixed_grad, log_totals, key_valid, block_rows, score_scale
):
    key_grad = jnp.zeros(key_rows.shape, jnp.float32)
    value_grad = jnp.zeros(value_rows.shape, jnp.float32)
    query_parts = []
    for row_start in range(0, query_rows.shape[0], block_rows):
        query_block = query_rows[row_start : row_start + block_rows]
        grad_block = mixed_grad[row_start : row_start + block_rows]
        scores = contract_last(query_block, key_rows) * score_scale
        scores = jnp.where(key_valid[None, :], scores, -jnp.inf)
        probs = jnp.exp(scores - log_totals[row_start : row_start + block_rows][:, None])
        prob_grad = contract_last(grad_block, value_rows)
        shared = jnp.sum(probs * prob_grad, axis=1, keepdims=True)
        score_grad = (probs * (prob_grad - shared)).astype(jnp.bfloat16)
        query_parts.append(
            jnp.dot(score_grad, key_rows, preferred_element_type=jnp.float32) * score_scale
        )
        key_grad = key_grad + contract_first(score_grad, query_block) * score_scale
        value_grad = value_grad + contract_first(probs.astype(jnp.bfloat16), grad_block)
    return (jnp.concatenate(query_parts, axis=0), key_grad, value_grad)


def per_device(
    x_in,
    cotangent,
    lengths,
    dealing,
    w_qkv,
    w_out,
    w_in,
    w_ffo,
    b_qv,
    b_out,
    b_in,
    b_ffo,
    ln1_gain,
    ln1_bias,
    ln2_gain,
    ln2_bias,
):
    owners = slot_owner(dealing)
    dealt_x, dealt_grad = (
        lax.all_to_all(
            jnp.take(x_in, owners, axis=0), "dp", split_axis=0, concat_axis=2, tiled=True
        ),
        lax.all_to_all(
            jnp.take(cotangent, owners, axis=0), "dp", split_axis=0, concat_axis=2, tiled=True
        ),
    )
    tokens_half = dealt_x[0, 0]
    output_grad = dealt_grad[0, 0].astype(jnp.float32)
    half_rows = tokens_half.shape[0]
    tensor_count = lax.axis_size("tensor")
    tensor_index = lax.axis_index("tensor")
    seq_rows = half_rows * tensor_count
    model_width = tokens_half.shape[1]
    head_width = b_qv.shape[1]
    head_count = head_width // HEAD_DIM
    ffn_width = b_in.shape[0]
    block_rows = min(512, seq_rows)
    score_scale = HEAD_DIM ** (-0.5)
    key_valid = jnp.arange(seq_rows) < lengths[lax.axis_index("dp")]
    qkv_weight, out_weight, in_weight, ffo_weight = (
        lax.all_gather(w_qkv.astype(jnp.bfloat16), "dp", axis=0, tiled=True),
        lax.all_gather(w_out.astype(jnp.bfloat16), "dp", axis=0, tiled=True),
        lax.all_gather(w_in.astype(jnp.bfloat16), "dp", axis=0, tiled=True),
        lax.all_gather(w_ffo.astype(jnp.bfloat16), "dp", axis=0, tiled=True),
    )

    def split_heads(matrix):
        return matrix.reshape(seq_rows, head_count, HEAD_DIM).transpose(1, 0, 2)

    def merge_heads(stacked):
        return stacked.transpose(1, 0, 2).reshape(seq_rows, head_width)

    tokens_full = lax.all_gather(tokens_half, "tensor", axis=0, tiled=True)
    projected = jnp.einsum(
        "ld,dce->cle", tokens_full, qkv_weight, preferred_element_type=jnp.float32
    )
    query_heads = split_heads((projected[0] + b_qv[0]).astype(jnp.bfloat16))
    key_heads = split_heads(projected[1].astype(jnp.bfloat16))
    value_heads = split_heads((projected[2] + b_qv[1]).astype(jnp.bfloat16))
    mixed_heads, log_totals = lax.map(
        lambda triple: head_forward(
            triple[0], triple[1], triple[2], key_valid, block_rows, score_scale
        ),
        (query_heads, key_heads, value_heads),
    )
    mixed_low = merge_heads(mixed_heads).astype(jnp.bfloat16)
    attn_half = lax.psum_scatter(
        contract_last(
            lax.slice_in_dim(mixed_low, 0, lax.axis_size("tensor") * half_rows, axis=0), out_weight
        ).astype(jnp.bfloat16),
        "tensor",
        scatter_dimension=0,
        tiled=True,
    ).astype(jnp.float32)
    first_norm, normed_one, inverse_one = norm_forward(
        tokens_half.astype(jnp.float32) + attn_half + b_out, ln1_gain, ln1_bias
    )
    first_full = lax.all_gather(first_norm.astype(jnp.bfloat16), "tensor", axis=0, tiled=True)
    hidden = jnp.dot(first_full, in_weight, preferred_element_type=jnp.float32) + b_in
    active = jax.nn.gelu(hidden, approximate=False).astype(jnp.bfloat16)
    ffn_half = lax.psum_scatter(
        contract_last(
            lax.slice_in_dim(active, 0, lax.axis_size("tensor") * half_rows, axis=0), ffo_weight
        ).astype(jnp.bfloat16),
        "tensor",
        scatter_dimension=0,
        tiled=True,
    ).astype(jnp.float32)
    result, normed_two, inverse_two = norm_forward(
        first_norm + ffn_half + b_ffo, ln2_gain, ln2_bias
    )
    final_grad, gain_two_grad, shift_two_grad = norm_backward(
        output_grad, normed_two, inverse_two, ln2_gain
    )
    ffo_bias_grad = jnp.sum(final_grad, axis=0)
    qkv_weight, out_weight, in_weight, ffo_weight = (
        lax.all_gather(w_qkv.astype(jnp.bfloat16), "dp", axis=0, tiled=True),
        lax.all_gather(w_out.astype(jnp.bfloat16), "dp", axis=0, tiled=True),
        lax.all_gather(w_in.astype(jnp.bfloat16), "dp", axis=0, tiled=True),
        lax.all_gather(w_ffo.astype(jnp.bfloat16), "dp", axis=0, tiled=True),
    )
    ffn_grad_full = lax.all_gather(final_grad.astype(jnp.bfloat16), "tensor", axis=0, tiled=True)
    ffo_weight_grad = contract_first(ffn_grad_full, active)
    hidden_grad = (
        jnp.dot(ffn_grad_full, ffo_weight, preferred_element_type=jnp.float32) * gelu_slope(hidden)
    ).astype(jnp.bfloat16)
    in_weight_grad = contract_first(first_full, hidden_grad)
    in_bias_grad = jnp.sum(hidden_grad.astype(jnp.float32), axis=0)
    first_grad = final_grad + lax.psum_scatter(
        contract_last(
            lax.slice_in_dim(hidden_grad, 0, lax.axis_size("tensor") * half_rows, axis=0), in_weight
        ).astype(jnp.bfloat16),
        "tensor",
        scatter_dimension=0,
        tiled=True,
    ).astype(jnp.float32)
    resid_grad, gain_one_grad, shift_one_grad = norm_backward(
        first_grad, normed_one, inverse_one, ln1_gain
    )
    out_bias_grad = jnp.sum(resid_grad, axis=0)
    attn_grad_full = lax.all_gather(resid_grad.astype(jnp.bfloat16), "tensor", axis=0, tiled=True)
    out_weight_grad = contract_first(attn_grad_full, mixed_low)
    mixed_grad = jnp.dot(attn_grad_full, out_weight, preferred_element_type=jnp.float32).astype(
        jnp.bfloat16
    )
    query_grads, key_grads, value_grads = lax.map(
        lambda bundle: head_backward(
            bundle[0],
            bundle[1],
            bundle[2],
            bundle[3],
            bundle[4],
            key_valid,
            block_rows,
            score_scale,
        ),
        (query_heads, key_heads, value_heads, split_heads(mixed_grad), log_totals),
    )
    qkv_grad = jnp.stack(
        [merge_heads(query_grads), merge_heads(key_grads), merge_heads(value_grads)]
    ).astype(jnp.bfloat16)
    qv_bias_grad = jnp.stack(
        [
            jnp.sum(qkv_grad[0].astype(jnp.float32), axis=0),
            jnp.sum(qkv_grad[2].astype(jnp.float32), axis=0),
        ]
    )
    qkv_weight_grad = jnp.einsum(
        "ld,cle->dce", tokens_full, qkv_grad, preferred_element_type=jnp.float32
    )
    rows_grad = lax.slice_in_dim(qkv_grad, 0, lax.axis_size("tensor") * half_rows, axis=1)
    input_grad = resid_grad + lax.psum_scatter(
        jnp.einsum("cle,dce->ld", rows_grad, qkv_weight, preferred_element_type=jnp.float32).astype(
            jnp.bfloat16
        ),
        "tensor",
        scatter_dimension=0,
        tiled=True,
    ).astype(jnp.float32)
    qkv_sum, out_sum, in_sum, ffo_sum = (
        lax.psum_scatter(qkv_weight_grad, "dp", scatter_dimension=0, tiled=True),
        lax.psum_scatter(out_weight_grad, "dp", scatter_dimension=0, tiled=True),
        lax.psum_scatter(in_weight_grad, "dp", scatter_dimension=0, tiled=True),
        lax.psum_scatter(ffo_weight_grad, "dp", scatter_dimension=0, tiled=True),
    )
    norm_terms = jnp.stack(
        [out_bias_grad, ffo_bias_grad, gain_one_grad, shift_one_grad, gain_two_grad, shift_two_grad]
    )
    qv_padded = lax.dynamic_update_slice_in_dim(
        jnp.zeros((2, model_width), jnp.float32), qv_bias_grad, tensor_index * head_width, 1
    )
    in_padded = lax.dynamic_update_slice_in_dim(
        jnp.zeros((ffn_width * tensor_count,), jnp.float32),
        in_bias_grad,
        tensor_index * ffn_width,
        0,
    )
    norm_sums, qv_sums, in_sums = lax.psum((norm_terms, qv_padded, in_padded), ("dp", "tensor"))
    qv_share = lax.dynamic_slice_in_dim(qv_sums, tensor_index * head_width, head_width, 1)
    in_share = lax.dynamic_slice_in_dim(in_sums, tensor_index * ffn_width, ffn_width, 0)
    back_out, back_grad = (
        lax.all_to_all(
            result.astype(jnp.bfloat16)[None, None], "dp", split_axis=2, concat_axis=0, tiled=True
        ),
        lax.all_to_all(
            input_grad.astype(jnp.bfloat16)[None, None],
            "dp",
            split_axis=2,
            concat_axis=0,
            tiled=True,
        ),
    )
    return (
        jnp.take(back_out, dealing, axis=0),
        jnp.take(back_grad, dealing, axis=0),
        qkv_sum,
        out_sum,
        in_sum,
        ffo_sum,
        qv_share,
        norm_sums[0],
        in_share,
        norm_sums[1],
        norm_sums[2],
        norm_sums[3],
        norm_sums[4],
        norm_sums[5],
    )


def solution(mesh):
    return jax.shard_map(
        per_device,
        mesh=mesh,
        in_specs=(
            P(None, "tensor", "dp", None),
            P(None, "tensor", "dp", None),
            P(),
            P(),
            P("dp", None, "tensor"),
            P("dp", "tensor"),
            P("dp", "tensor"),
            P("dp", "tensor"),
            P(None, "tensor"),
            P(),
            P("tensor"),
            P(),
            P(),
            P(),
            P(),
            P(),
        ),
        out_specs=(
            P(None, "tensor", "dp", None),
            P(None, "tensor", "dp", None),
            P("dp", None, "tensor"),
            P("dp", "tensor"),
            P("dp", "tensor"),
            P("dp", "tensor"),
            P(None, "tensor"),
            P(),
            P("tensor"),
            P(),
            P(),
            P(),
            P(),
            P(),
        ),
        check_vma=False,
    )
```

profile of v0, /device:TPU:0, one launch (start us, length us, event | category | flops | bytes accessed | tf_op | source)
XLA Modules:
  0.0 1286.9 jit_solution(3330152919851395239)
XLA Ops:
  16.4 53.0 %all_to_all.42 = bf16[16,1,64,768]{3,2,1,0:T(8,128)(2,1)} all-to-all(bf16[16,1,64,768]{3,2,1,0:T(8,128)(2,1)S(1)} %get-tuple-element.272), channel_id=1, replica_groups=mesh['dp'=16,'tensor'=2] {'dp'}, dimensions={0} | all-to-all | bytes 3145728 | tf_op jit(solution)/shard_map/all_to_all | solution.py:112
  70.2 23.6 %all_gather.30 = bf16[768,384]{1,0:T(8,128)(2,1)} all-gather(bf16[48,384]{1,0:T(8,128)(2,1)S(1)} %convert_element_type.160), channel_id=1, replica_groups=mesh['dp'=16,'tensor'=2] {'dp'}, dimensions={0}, use_global_device_ids=true | all-gather | bytes 626688 | tf_op jit(solution)/shard_map/all_gather | solution.py:134
  93.8 20.8 %all-gather.8.cloned.1.call-done = bf16[2048,768]{1,0:T(8,128)(2,1)} async-done(((bf16[1024,768]{1,0:T(8,128)(2,1)}), bf16[2048,768]{1,0:T(8,128)(2,1)}) %all-gather.8.cloned.1.call-update) | async-done | bytes 3145744 | tf_op jit(solution)/shard_map/all_gather | solution.py:145
  114.7 6.5 convolution_bitcast_fusion
  122.5 3.0 fusion.154
  125.6 3.1 copy.69
  128.6 5.8 copy.68
  134.4 5.7 copy.70
  140.1 5.2 fusion.129
  148.9 117.0 %while.28 = (s32[]{:T(128)}, bf16[6,2048,64]{1,2,0:T(8,128)(2,1)}, f32[6,2048]{1,0:T(8,128)}, bf16[6,2048,64]{2,1,0:T(8,128)(2,1)}, bf16[6,2048,64]{2,1,0:T(8,12...) while((s32[]{:T(128)}, bf16[6,2048,64]{1,2,0:T(8,128)(2,1)}, ...), condition=%wide.region_10.12_spmd.clone, body=%wide.region_1.11_spmd.clone.sunk | while | flops 1125128192 | bytes 70637272 | solution.py:152
  155.0 3.5 fusion.240
  159.8 2.9 fusion.241
  174.4 3.5 fusion.240
  179.2 2.9 fusion.241
  193.8 3.5 fusion.240
  198.6 2.9 fusion.241
  213.2 3.5 fusion.240
  218.0 2.9 fusion.241
  232.6 3.5 fusion.240
  237.4 2.9 fusion.241
  252.0 3.5 fusion.240
  256.8 2.9 fusion.241
  265.9 6.2 convolution_convert_fusion
  273.8 41.9 %reduce-scatter.9.cloned.1.call-done = bf16[1024,768]{1,0:T(8,128)(2,1)} async-done(((bf16[2048,768]{1,0:T(8,128)(2,1)}), bf16[1024,768]{1,0:T(8,128)(2,1)}) %reduce-scatter.9.cloned.1.call-update) | async-done | bytes 1572880 | tf_op jit(solution)/shard_map/reduce_scatter | solution.py:159
  321.6 39.1 %all-gather.14.cloned.1.call-done = bf16[768,1536]{1,0:T(8,128)(2,1)} async-done(((bf16[48,1536]{1,0:T(8,128)(2,1)}), bf16[768,1536]{1,0:T(8,128)(2,1)}) %all-gather.14.cloned.1.call-update) | async-done | bytes 2359312 | tf_op jit(solution)/shard_map/all_gather | solution.py:135
  360.7 45.1 %all-gather.12.cloned.1.call-done = bf16[2048,768]{1,0:T(8,128)(2,1)} async-done(((bf16[1024,768]{1,0:T(8,128)(2,1)}), bf16[2048,768]{1,0:T(8,128)(2,1)}) %all-gather.12.cloned.1.call-update) | async-done | bytes 3145744 | tf_op jit(solution)/shard_map/all_gather | solution.py:170
  405.8 34.6 %fusion.115 = (bf16[2048,1536]{1,0:T(8,128)(2,1)}, f32[2048,1536]{1,0:T(8,128)}) fusion(f32[1536]{0:T(1024)S(1)} %copy-done.49, bf16[2048,768]{1,0:T(8,128)(2,1)} %all-gather.12.cloned.1.call-done, bf16[768,1536]{1,0:T(8,128)(2,1)} %all-gather.14.cloned.1.call-done), kind=kOutput, calls=%fused_computation.175 | convolution fusion | flops 5039456256 | bytes 24385536 | tf_op jit(solution)/shard_map/dot_general | solution.py:171
  440.4 10.5 all-gather.16.cloned.1.call-done
  450.8 9.0 convolution_convert_fusion.2
  460.0 40.0 %all_to_all.43 = bf16[16,1,64,768]{3,2,1,0:T(8,128)(2,1)S(1)} all-to-all(bf16[16,1,64,768]{3,2,1,0:T(8,128)(2,1)} %get-tuple-element.271), channel_id=1, replica_groups=mesh['dp'=16,'tensor'=2] {'dp'}, dimensions={0} | all-to-all | bytes 3145728 | tf_op jit(solution)/shard_map/all_to_all | solution.py:115
  502.5 2.9 fusion.153
  508.6 3.4 fusion.151
  512.0 45.3 %all-gather.18.cloned.1.call-done = bf16[2048,768]{1,0:T(8,128)(2,1)} async-done(((bf16[1024,768]{1,0:T(8,128)(2,1)}), bf16[2048,768]{1,0:T(8,128)(2,1)}) %all-gather.18.cloned.1.call-update) | async-done | bytes 3145744 | tf_op jit(solution)/shard_map/all_gather | solution.py:194
  557.3 12.4 convert_reduce_fusion
  572.3 6.4 convolution_convert_fusion.1
  578.8 43.5 %reduce-scatter.13.cloned.1.call-done = bf16[1024,768]{1,0:T(8,128)(2,1)} async-done(((bf16[2048,768]{1,0:T(8,128)(2,1)}), bf16[1024,768]{1,0:T(8,128)(2,1)}) %reduce-scatter.13.cloned.1.call-update) | async-done | bytes 1572880 | tf_op jit(solution)/shard_map/reduce_scatter | solution.py:201
  622.4 4.6 multiply_reduce_fusion.4
  632.4 45.0 %all-gather.20.cloned.1.call-done = bf16[2048,768]{1,0:T(8,128)(2,1)} async-done(((bf16[1024,768]{1,0:T(8,128)(2,1)}), bf16[2048,768]{1,0:T(8,128)(2,1)}) %all-gather.20.cloned.1.call-update) | async-done | bytes 3145744 | tf_op jit(solution)/shard_map/all_gather | solution.py:213
  677.4 3.3 convolution_convert_fusion.3
  680.8 2.9 copy.72
  687.6 217.3 %while.29 = (s32[]{:T(128)}, bf16[6,2048,64]{1,2,0:T(8,128)(2,1)}, bf16[6,2048,64]{1,2,0:T(8,128)(2,1)}, bf16[6,2048,64]{1,2,0:T(8,128)(2,1)}, bf16[6,2048,64]{2...) while((s32[]{:T(128)}, bf16[6,2048,64]{1,2,0:T(8,128)(2,1)}, ...), condition=%wide.region_27.29_spmd.clone, body=%wide.region_22.28_spmd.clone.sunk | while | flops 2724331520 | bytes 161284432 | solution.py:218
  910.9 8.5 bitcast_convert_fusion
  921.3 9.6 fusion.157
  932.8 9.5 fusion.156
  943.7 4.8 fusion.155
  948.5 3.8 copy.87
  952.8 11.5 reduce.24
  964.3 4.7 reshape.275
  969.0 5.7 all-to-all-start.1
  974.7 8.7 fusion.138
  989.8 11.5 reduce.23
  1001.3 4.6 reshape.277
  1005.9 9.2 all-to-all-done.1
  1015.1 19.2 %all-to-all-start.3 = ((bf16[16,2,24576]{2,1,0:T(2,128)(2,1)}), bf16[16,2,24576]{2,1,0:T(2,128)(2,1)}, u32[]{:S(2)}, u32[]{:S(2)}) async-start(bf16[16,2,24576]{2,1,0:T(2,128)(2,1)} %reshape.277), calls=%async_computation.7 | async-start | bytes 3145728 | tf_op jit(solution)/shard_map/all_to_all | solution.py:277
  1034.4 10.1 reshape.276
  1044.5 3.4 copy.82
  1047.9 3.3 gather_fusion.1
  1052.3 48.6 %all-reduce = (f32[2,768]{1,0:T(2,128)S(1)}, f32[6,768]{1,0:T(8,128)S(1)}, f32[3072]{0:T(1024)S(1)}) all-reduce(f32[2,768]{1,0:T(2,128)S(1)} %maximum_dynamic-update-slice_fusion, f32[6,768]{1,0:T(8,128)S(1)} %stack.44, f32[3072]{0:T(1024)S(1)} %dynamic_update_slice.24), channel_id=1, replica_groups=mesh['dp'=16,'tensor'=2] {'dp','tensor'}, use_global_device_ids=true, to_apply=%region_35.37 | all-reduce | flops 9216 | bytes 73728 | tf_op jit(solution)/shard_map/psum | solution.py:270
  1102.8 8.1 reshape.278
  1112.3 3.3 gather_fusion.3
  1115.7 3.5 fusion.145
  1119.2 28.1 %reduce-scatter.21.cloned.1.call-done = f32[48,1536]{1,0:T(8,128)} async-done(((f32[768,1536]{1,0:T(8,128)}), f32[48,1536]{1,0:T(8,128)}) %reduce-scatter.21.cloned.1.call-update) | async-done | bytes 294928 | tf_op jit(solution)/shard_map/reduce_scatter | solution.py:255
  1147.3 61.5 %reduce-scatter.19.cloned.1.call-done = f32[48,384]{1,0:T(8,128)} async-done(((f32[768,384]{1,0:T(8,128)}), f32[48,384]{1,0:T(8,128)}) %reduce-scatter.19.cloned.1.call-update) | async-done | bytes 73744 | tf_op jit(solution)/shard_map/reduce_scatter | solution.py:254
  1208.7 71.4 %reduce-scatter.17.cloned.1.call-done = f32[48,3,384]{2,0,1:T(8,128)} async-done(((f32[768,3,384]{2,0,1:T(8,128)}), f32[48,3,384]{2,0,1:T(8,128)}) %reduce-scatter.17.cloned.1.call-update) | async-done | bytes 221200 | tf_op jit(solution)/shard_map/reduce_scatter | solution.py:253
  (484 shorter events, 356.2 us)
Async XLA Ops:
  7.2 5.0 copy-start
  7.2 86.6 %all-gather.10.cloned.1.call-start = ((), (), s32[]{:S(2)}) async-start(), calls=%async_computation.13 | async-start | bytes 1880064 | tf_op jit(solution)/shard_map/all_gather | solution.py:133
  9.0 105.7 %all-gather.8.cloned.1.call-start = ((), (), s32[]{:S(2)}) async-start(), calls=%async_computation.12 | async-start | bytes 4718592 | tf_op jit(solution)/shard_map/all_gather | solution.py:145
  16.4 53.1 %copy-start.43 = (f32[2,384]{1,0:T(2,128)S(1)}, f32[2,384]{1,0:T(2,128)}, u32[]{:S(2)}) copy-start(f32[2,384]{1,0:T(2,128)} %param.30) | copy-start | bytes 9220
  16.4 53.3 %copy-start.30 = (f32[48,384]{1,0:T(8,128)S(1)}, f32[48,384]{1,0:T(8,128)}, u32[]{:S(2)}) copy-start(f32[48,384]{1,0:T(8,128)} %param.27) | copy-start | bytes 221188
  16.4 53.3 %copy-start.50 = (s32[16]{0:T(128)S(1)}, s32[16]{0:T(128)}, u32[]{:S(2)}) copy-start(s32[16]{0:T(128)} %param.24) | copy-start | bytes 196
  69.4 246.3 %reduce-scatter.9.cloned.1.call-start = ((), (), s32[]{:S(2)}) async-start(), calls=%async_computation.14 | async-start | bytes 4718592 | tf_op jit(solution)/shard_map/reduce_scatter | solution.py:159
  140.1 5.2 copy-start.11
  155.0 3.5 copy-start.5
  174.4 3.5 copy-start.5
  193.8 3.5 copy-start.5
  213.2 3.5 copy-start.5
  232.6 3.5 copy-start.5
  252.0 3.5 copy-start.5
  265.9 6.2 copy-start.2
  272.0 43.6 %copy-start.29 = (f32[768]{0:T(1024)S(1)}, f32[768]{0:T(1024)}, u32[]{:S(2)}) copy-start(f32[768]{0:T(1024)} %param.31) | copy-start | bytes 9220
  272.0 43.6 %copy-start.4 = (bf16[16,1,64,768]{3,2,1,0:T(8,128)(2,1)S(1)}, bf16[16,1,64,768]{3,2,1,0:T(8,128)(2,1)}, u32[]{:S(2)}) copy-start(bf16[16,1,64,768]{3,2,1,0:T(8,128)(2,1)} %all_to_all.42) | copy-start | bytes 4718596
  272.1 88.6 %all-gather.14.cloned.1.call-start = ((), (), s32[]{:S(2)}) async-start(), calls=%async_computation.16 | async-start | bytes 2506752 | tf_op jit(solution)/shard_map/all_gather | solution.py:135
  273.7 45.0 %copy-start.31 = (f32[768]{0:T(1024)S(1)}, f32[768]{0:T(1024)}, u32[]{:S(2)}) copy-start(f32[768]{0:T(1024)} %param.34) | copy-start | bytes 9220
  273.7 45.0 %copy-start.38 = (f32[768]{0:T(1024)S(1)}, f32[768]{0:T(1024)}, u32[]{:S(2)}) copy-start(f32[768]{0:T(1024)} %param.35) | copy-start | bytes 9220
  273.7 132.0 %all-gather.12.cloned.1.call-start = ((), (), s32[]{:S(2)}) async-start(), calls=%async_computation.15 | async-start | bytes 4718592 | tf_op jit(solution)/shard_map/all_gather | solution.py:170
  318.7 87.1 %copy-start.49 = (f32[1536]{0:T(1024)S(1)}, f32[1536]{0:T(1024)}, u32[]{:S(2)}) copy-start(f32[1536]{0:T(1024)} %param.32) | copy-start | bytes 18436
  320.8 130.0 %all-gather.16.cloned.1.call-start = ((), (), s32[]{:S(2)}) async-start(), calls=%async_computation.17 | async-start | bytes 2506752 | tf_op jit(solution)/shard_map/all_gather | solution.py:136
  321.6 180.9 %reduce-scatter.11.cloned.1.call-start = ((), (), s32[]{:S(2)}) async-start(), calls=%async_computation.18 | async-start | bytes 4718592 | tf_op jit(solution)/shard_map/reduce_scatter | solution.py:173
  459.9 41.2 %copy-start.32 = (f32[768]{0:T(1024)S(1)}, f32[768]{0:T(1024)}, u32[]{:S(2)}) copy-start(f32[768]{0:T(1024)} %param.36) | copy-start | bytes 9220
  459.9 42.6 %copy-start.41 = (f32[768]{0:T(1024)S(1)}, f32[768]{0:T(1024)}, u32[]{:S(2)}) copy-start(f32[768]{0:T(1024)} %param.33) | copy-start | bytes 9220
  459.9 97.4 %all-gather.18.cloned.1.call-start = ((), (), s32[]{:S(2)}) async-start(), calls=%async_computation.19 | async-start | bytes 4718592 | tf_op jit(solution)/shard_map/all_gather | solution.py:194
  512.0 110.4 %reduce-scatter.13.cloned.1.call-start = ((), (), s32[]{:S(2)}) async-start(), calls=%async_computation.20 | async-start | bytes 4718592 | tf_op jit(solution)/shard_map/reduce_scatter | solution.py:201
  557.3 15.1 %copy-start.48 = (bf16[768,1536]{1,0:T(8,128)(2,1)S(1)}, bf16[768,1536]{1,0:T(8,128)(2,1)}, u32[]{:S(2)}) copy-start(bf16[768,1536]{1,0:T(8,128)(2,1)} %all-gather.14.cloned.1.call-done) | copy-start | bytes 7077892
  578.8 98.7 %all-gather.20.cloned.1.call-start = ((), (), s32[]{:S(2)}) async-start(), calls=%async_computation.21 | async-start | bytes 4718592 | tf_op jit(solution)/shard_map/all_gather | solution.py:213
  622.4 4.6 copy-start.10
  622.4 4.6 copy-start.21
  631.1 46.4 %copy-start.26 = (bf16[768,384]{1,0:T(8,128)(2,1)S(1)}, bf16[768,384]{1,0:T(8,128)(2,1)}, u32[]{:S(2)}) copy-start(bf16[768,384]{1,0:T(8,128)(2,1)} %all_gather.30) | copy-start | bytes 1769476
  632.4 351.1 %reduce-scatter.15.cloned.1.call-start = ((), (), s32[]{:S(2)}) async-start(), calls=%async_computation.22 | async-start | bytes 4718592 | tf_op jit(solution)/shard_map/reduce_scatter | solution.py:244
  683.6 4.0 copy-start.3
  687.8 3.6 copy-start.6
  724.0 3.6 copy-start.6
  760.1 3.6 copy-start.6
  796.2 3.6 copy-start.6
  832.4 3.6 copy-start.6
  868.5 3.6 copy-start.6
  904.9 2.8 copy-start.16
  904.9 4.4 copy-start.14
  919.5 199.7 %reduce-scatter.23.cloned.1.call-start = ((), (), s32[]{:S(2)}) async-start(), calls=%async_computation.26 | async-start | bytes 5013504 | tf_op jit(solution)/shard_map/reduce_scatter | solution.py:256
  930.9 216.3 %reduce-scatter.21.cloned.1.call-start = ((), (), s32[]{:S(2)}) async-start(), calls=%async_computation.25 | async-start | bytes 5013504 | tf_op jit(solution)/shard_map/reduce_scatter | solution.py:255
  942.3 266.4 %reduce-scatter.19.cloned.1.call-start = ((), (), s32[]{:S(2)}) async-start(), calls=%async_computation.24 | async-start | bytes 1253376 | tf_op jit(solution)/shard_map/reduce_scatter | solution.py:254
  964.3 10.4 copy-start.23
  964.3 10.4 copy-start.24
  969.0 46.1 %all-to-all-start.1 = ((bf16[16,2,24576]{2,1,0:T(2,128)(2,1)}), bf16[16,2,24576]{2,1,0:T(2,128)(2,1)}, u32[]{:S(2)}, u32[]{:S(2)}) async-start(bf16[16,2,24576]{2,1,0:T(2,128)(2,1)} %reshape.275), calls=%async_computation.3 | async-start | bytes 3145728 | tf_op jit(solution)/shard_map/all_to_all | solution.py:274
  974.7 305.5 %reduce-scatter.17.cloned.1.call-start = ((), (), s32[]{:S(2)}) async-start(), calls=%async_computation.23 | async-start | bytes 3760128 | tf_op jit(solution)/shard_map/reduce_scatter | solution.py:253
  1001.3 33.0 %copy-start.45 = (s32[16]{0:T(128)S(1)}, s32[16]{0:T(128)}, u32[]{:S(2)}) copy-start(s32[16]{0:T(128)} %get-tuple-element.277) | copy-start | bytes 196
  1001.3 33.0 %copy-start.36 = (f32[768]{0:T(1024)S(1)}, f32[768]{0:T(1024)}, u32[]{:S(2)}) copy-start(f32[768]{0:T(1024)} %get-tuple-element.194) | copy-start | bytes 9220
  1001.3 33.1 %copy-start.39 = (f32[768]{0:T(1024)S(1)}, f32[768]{0:T(1024)}, u32[]{:S(2)}) copy-start(f32[768]{0:T(1024)} %get-tuple-element.189) | copy-start | bytes 9220
  1015.1 87.7 %all-to-all-start.3 = ((bf16[16,2,24576]{2,1,0:T(2,128)(2,1)}), bf16[16,2,24576]{2,1,0:T(2,128)(2,1)}, u32[]{:S(2)}, u32[]{:S(2)}) async-start(bf16[16,2,24576]{2,1,0:T(2,128)(2,1)} %reshape.277), calls=%async_computation.7 | async-start | bytes 3145728 | tf_op jit(solution)/shard_map/all_to_all | solution.py:277
  1044.5 6.8 copy-start.40
  1044.5 7.1 copy-start.35
  1044.5 7.1 copy-start.34
  1044.5 7.1 copy-start.33
  1044.5 7.1 copy-start.37
  1044.5 7.2 copy-start.17
  1047.9 4.0 copy-start.15
  1110.9 4.7 copy-start.44
  1112.3 3.3 copy-start.20
  1115.7 164.5 %copy-start.1 = (bf16[16,1,64,768]{3,2,1,0:T(8,128)(2,1)S(1)}, bf16[16,1,64,768]{3,2,1,0:T(8,128)(2,1)}, u32[]{:S(2)}) copy-start(bf16[16,1,64,768]{3,2,1,0:T(8,128)(2,1)} %param.23) | copy-start | bytes 4718596
  (25 other events, 44.9 us)
Sparse Core Ops, SparseCore 0:
  10.9 53.5 all-gather.9
  69.5 45.1 all-gather.7
  272.2 43.4 reduce-scatter.8
  318.4 42.2 all-gather.13
  362.1 43.6 all-gather.11
  408.5 42.2 all-gather.15
  460.0 42.1 reduce-scatter.10
  512.1 45.1 all-gather.17
  578.9 43.4 reduce-scatter.12
  632.5 44.8 all-gather.19
  919.6 43.4 reduce-scatter.14
  967.3 94.5 reduce-scatter.22
  1066.4 80.8 reduce-scatter.20
  1151.3 57.3 reduce-scatter.18
  1213.0 67.1 reduce-scatter.16
where the time goes:
time: 1300 us; the launch traced here: 1290 us
  waiting for transfers between devices  462 us (36%)
  matrix products  388 us (30%)
  blocking collectives  165 us (13%)
  local copies, waits for them, and re-layouts  116 us (9%)
  other arithmetic  113 us (9%)
  starting transfers between devices  25.9 us (2%)
  between operations  14.7 us (1%)
    dot_general x75, matrix products, contract_last(): lax.dot_general(left_side, right_side, (((1,), (1,)), ((), ())), preferre...  168 us
    dot_general x51, matrix products, contract_first(): lax.dot_general(left_side, right_side, (((0,), (0,)), ((), ())), preferre...  97.7 us
    reduce_scatter x1, waiting for transfers between devices, per_device(): lax.psum_scatter(qkv_weight_grad, 'dp', scatter_dimension=0, tiled=True)  71.4 us
    reduce_scatter x1, waiting for transfers between devices, per_device(): lax.psum_scatter(out_weight_grad, 'dp', scatter_dimension=0, tiled=True)  61.5 us
    all_to_all x1, blocking collectives, per_device(): lax.all_to_all(jnp.take(x_in, owners, axis=0), 'dp', split_axis=0, concat...  53 us
    psum x1, blocking collectives, per_device(): lax.psum((norm_terms, qv_padded, in_padded), ('dp', 'tensor'))  48.6 us
    unnamed x103, local copies, waits for them, and re-layouts  46.6 us
    all_gather x1, waiting for transfers between devices, per_device(): lax.all_gather(final_grad.astype(jnp.bfloat16), 'tensor', axis=0, tiled=T...  45.3 us
  transfers between devices with their start and end apart: 17, of which 12 were waited for; matrix products, arithmetic and copies ran while one was open for 12% of the time, Pallas kernels for 0%

commit v1 on v0

--- a/solution.py
+++ b/solution.py
@@ -1,9 +1,40 @@
+import functools
 import jax
 import jax.numpy as jnp
 from jax import lax
 from jax.sharding import PartitionSpec as P
 
 HEAD_DIM = 64
+
+
+def try_all_the_patches(u_in, axis_k, work_x):
+    base_arr = u_in.shape
+    z = u_in.reshape(
+        *base_arr[:axis_k], work_x, base_arr[axis_k] // work_x, *base_arr[axis_k + 1 :]
+    )
+    return jnp.moveaxis(z, axis_k, 0)
+
+
+def step_on_tracks(vec, d0):
+    vec = jnp.moveaxis(vec, 0, d0)
+    t1 = vec.shape
+    return vec.reshape(*t1[:d0], t1[d0] * t1[d0 + 1], *t1[d0 + 2 :])
+
+
+def update_the_pages(inputs, net_axis, local_array, point):
+    long_array = lax.axis_size(net_axis)
+    z1, local_next = (long_array, lax.axis_index(net_axis))
+    passed = try_all_the_patches(inputs, local_array, z1)
+    column = [passed[local_next]]
+    for tick in range(1, z1):
+        after = passed[(local_next + tick) % z1]
+        e_next = lax.ppermute(after, net_axis, [(dd, (dd + tick) % z1) for dd in range(z1)])
+        column.append(e_next)
+    passed = jnp.stack(column, axis=0)[(local_next - jnp.arange(z1)) % z1]
+    return step_on_tracks(passed, point)
+
+
+fill_thing = functools.partial(update_the_pages, net_axis="dp", local_array=0, point=2)
 
 
 def slot_owner(dealing):
@@ -109,9 +140,7 @@
 ):
     owners = slot_owner(dealing)
     dealt_x, dealt_grad = (
-        lax.all_to_all(
-            jnp.take(x_in, owners, axis=0), "dp", split_axis=0, concat_axis=2, tiled=True
-        ),
+        fill_thing(jnp.take(x_in, owners, axis=0)),
         lax.all_to_all(
             jnp.take(cotangent, owners, axis=0), "dp", split_axis=0, concat_axis=2, tiled=True
         ),

time: 1300 us -> 1370 us (1.054)
  waiting for transfers between devices: 462 us -> 561 us
  blocking collectives: 165 us -> 115 us
    ppermute x0 -> x15, waiting for transfers between devices: none -> 57.3 us  [update_the_pages(): lax.ppermute(after, net_axis, [(dd, (dd + tick) % z1) for dd in range(z1)])]
    all_to_all x1 -> x0, blocking collectives: 53 us -> none  [per_device(): lax.all_to_all(jnp.take(x_in, owners, axis=0), 'dp', split_axis=0, concat...]
    all_gather x1, waiting for transfers between devices: 0.01 us -> 43.4 us  [per_device(): lax.all_gather(w_qkv.astype(jnp.bfloat16), 'dp', axis=0, tiled=True)]
    unnamed x103 -> x124, local copies, waits for them, and re-layouts: 46.6 us -> 50.1 us
  transfers between devices with their start and end apart: 17 -> 32, of which waited for: 12 -> 24; matrix products, arithmetic and copies ran while one was open for 12% -> 12% of each run, Pallas kernels for 0% -> 0%
where the time goes in v1:
time: 1370 us; the launch traced here: 1350 us
  waiting for transfers between devices  561 us (41%)
  matrix products  388 us (28%)
  local copies, waits for them, and re-layouts  123 us (9%)
  blocking collectives  115 us (8%)
  other arithmetic  112 us (8%)
  starting transfers between devices  37.9 us (3%)
  between operations  15 us (1%)
    dot_general x75, matrix products, contract_last(): lax.dot_general(left_side, right_side, (((1,), (1,)), ((), ())), preferre...  168 us
    dot_general x51, matrix products, contract_first(): lax.dot_general(left_side, right_side, (((0,), (0,)), ((), ())), preferre...  97.7 us
    reduce_scatter x1, waiting for transfers between devices, per_device(): lax.psum_scatter(qkv_weight_grad, 'dp', scatter_dimension=0, tiled=True)  71.6 us
    reduce_scatter x1, waiting for transfers between devices, per_device(): lax.psum_scatter(out_weight_grad, 'dp', scatter_dimension=0, tiled=True)  61.4 us
    ppermute x15, waiting for transfers between devices, update_the_pages(): lax.ppermute(after, net_axis, [(dd, (dd + tick) % z1) for dd in range(z1)])  57.3 us
    unnamed x124, local copies, waits for them, and re-layouts  50.1 us
    psum x1, blocking collectives, per_device(): lax.psum((norm_terms, qv_padded, in_padded), ('dp', 'tensor'))  48.6 us
    all_gather x1, waiting for transfers between devices, per_device(): lax.all_gather(first_norm.astype(jnp.bfloat16), 'tensor', axis=0, tiled=T...  45.6 us
  transfers between devices with their start and end apart: 32, of which 24 were waited for; matrix products, arithmetic and copies ran while one was open for 12% of the time, Pallas kernels for 0%

profile of v1, /device:TPU:0, one launch (start us, length us, event | category | flops | bytes accessed | tf_op | source)
XLA Modules:
  0.0 1354.6 jit_solution(13086367192912462280)
XLA Ops:
  10.7 5.5 collective-permute-start.14
  19.8 5.1 collective-permute-done
  25.8 6.4 collective-permute-done.1
  32.2 5.8 collective-permute-done.2
  38.0 6.4 collective-permute-done.3
  44.4 5.8 collective-permute-done.4
  50.3 6.4 collective-permute-done.5
  56.7 5.6 collective-permute-done.6
  62.3 5.5 collective-permute-done.7
  67.8 4.9 collective-permute-done.8
  85.9 27.4 %all_gather.30 = bf16[768,384]{1,0:T(8,128)(2,1)} all-gather(bf16[48,384]{1,0:T(8,128)(2,1)S(1)} %convert_element_type.160), channel_id=1, replica_groups=mesh['dp'=16,'tensor'=2] {'dp'}, dimensions={0}, use_global_device_ids=true | all-gather | bytes 626688 | tf_op jit(solution)/shard_map/all_gather | solution.py:163
  113.2 20.3 %all-gather.8.cloned.1.call-done = bf16[2048,768]{1,0:T(8,128)(2,1)} async-done(((bf16[1024,768]{1,0:T(8,128)(2,1)}), bf16[2048,768]{1,0:T(8,128)(2,1)}) %all-gather.8.cloned.1.call-update) | async-done | bytes 3145744 | tf_op jit(solution)/shard_map/all_gather | solution.py:174
  133.6 43.4 %all-gather.10.cloned.1.call-done = bf16[768,3,384]{2,0,1:T(8,128)(2,1)} async-done(((bf16[48,3,384]{2,0,1:T(8,128)(2,1)}), bf16[768,3,384]{2,0,1:T(8,128)(2,1)}) %all-gather.10.cloned.1.call-update) | async-done | bytes 1769488 | tf_op jit(solution)/shard_map/all_gather | solution.py:162
  176.9 6.5 convolution_bitcast_fusion
  190.9 5.8 copy.138
  196.6 5.7 copy.140
  202.4 8.7 fusion.129
  212.4 117.0 %while.28 = (s32[]{:T(128)}, bf16[6,2048,64]{1,2,0:T(8,128)(2,1)}, f32[6,2048]{1,0:T(8,128)}, bf16[6,2048,64]{2,1,0:T(8,128)(2,1)}, bf16[6,2048,64]{2,1,0:T(8,12...) while((s32[]{:T(128)}, bf16[6,2048,64]{1,2,0:T(8,128)(2,1)}, ...), condition=%wide.region_10.12_spmd.clone, body=%wide.region_1.11_spmd.clone.sunk | while | flops 1125128192 | bytes 70637272 | solution.py:181
  218.5 3.5 fusion.243
  237.9 3.5 fusion.243
  257.3 3.5 fusion.243
  276.7 3.5 fusion.243
  296.1 3.5 fusion.243
  315.5 3.5 fusion.243
  329.4 6.2 convolution_convert_fusion
  337.3 40.6 %reduce-scatter.9.cloned.1.call-done = bf16[1024,768]{1,0:T(8,128)(2,1)} async-done(((bf16[2048,768]{1,0:T(8,128)(2,1)}), bf16[1024,768]{1,0:T(8,128)(2,1)}) %reduce-scatter.9.cloned.1.call-update) | async-done | bytes 1572880 | tf_op jit(solution)/shard_map/reduce_scatter | solution.py:188
  383.8 39.1 %all-gather.14.cloned.1.call-done = bf16[768,1536]{1,0:T(8,128)(2,1)} async-done(((bf16[48,1536]{1,0:T(8,128)(2,1)}), bf16[768,1536]{1,0:T(8,128)(2,1)}) %all-gather.14.cloned.1.call-update) | async-done | bytes 2359312 | tf_op jit(solution)/shard_map/all_gather | solution.py:164
  422.9 45.6 %all-gather.12.cloned.1.call-done = bf16[2048,768]{1,0:T(8,128)(2,1)} async-done(((bf16[1024,768]{1,0:T(8,128)(2,1)}), bf16[2048,768]{1,0:T(8,128)(2,1)}) %all-gather.12.cloned.1.call-update) | async-done | bytes 3145744 | tf_op jit(solution)/shard_map/all_gather | solution.py:199
  468.5 34.6 %fusion.115 = (bf16[2048,1536]{1,0:T(8,128)(2,1)}, f32[2048,1536]{1,0:T(8,128)}) fusion(f32[1536]{0:T(1024)S(1)} %copy-done.51, bf16[2048,768]{1,0:T(8,128)(2,1)} %all-gather.12.cloned.1.call-done, bf16[768,1536]{1,0:T(8,128)(2,1)} %all-gather.14.cloned.1.call-done), kind=kOutput, calls=%fused_computation.176 | convolution fusion | flops 5039456256 | bytes 24385536 | tf_op jit(solution)/shard_map/dot_general | solution.py:200
  503.1 10.4 all-gather.16.cloned.1.call-done
  513.6 9.0 convolution_convert_fusion.2
  522.7 3.3 gather_fusion.3
  527.7 39.5 %all_to_all.33 = bf16[16,1,64,768]{3,2,1,0:T(8,128)(2,1)S(1)} all-to-all(bf16[16,1,64,768]{3,2,1,0:T(8,128)(2,1)S(1)} %bitcast_select_fusion.1), channel_id=1, replica_groups=mesh['dp'=16,'tensor'=2] {'dp'}, dimensions={0} | all-to-all | bytes 3145728 | tf_op jit(solution)/shard_map/all_to_all | solution.py:144
  575.9 3.4 fusion.153
  579.3 45.4 %all-gather.18.cloned.1.call-done = bf16[2048,768]{1,0:T(8,128)(2,1)} async-done(((bf16[1024,768]{1,0:T(8,128)(2,1)}), bf16[2048,768]{1,0:T(8,128)(2,1)}) %all-gather.18.cloned.1.call-update) | async-done | bytes 3145744 | tf_op jit(solution)/shard_map/all_gather | solution.py:223
  624.7 12.4 convert_reduce_fusion
  639.8 6.4 convolution_convert_fusion.1
  646.3 43.5 %reduce-scatter.13.cloned.1.call-done = bf16[1024,768]{1,0:T(8,128)(2,1)} async-done(((bf16[2048,768]{1,0:T(8,128)(2,1)}), bf16[1024,768]{1,0:T(8,128)(2,1)}) %reduce-scatter.13.cloned.1.call-update) | async-done | bytes 1572880 | tf_op jit(solution)/shard_map/reduce_scatter | solution.py:230
  689.8 4.6 multiply_reduce_fusion.4
  699.9 45.0 %all-gather.20.cloned.1.call-done = bf16[2048,768]{1,0:T(8,128)(2,1)} async-done(((bf16[1024,768]{1,0:T(8,128)(2,1)}), bf16[2048,768]{1,0:T(8,128)(2,1)}) %all-gather.20.cloned.1.call-update) | async-done | bytes 3145744 | tf_op jit(solution)/shard_map/all_gather | solution.py:242
  755.1 217.3 %while.29 = (s32[]{:T(128)}, bf16[6,2048,64]{1,2,0:T(8,128)(2,1)}, bf16[6,2048,64]{1,2,0:T(8,128)(2,1)}, bf16[6,2048,64]{1,2,0:T(8,128)(2,1)}, bf16[6,2048,64]{2...) while((s32[]{:T(128)}, bf16[6,2048,64]{1,2,0:T(8,128)(2,1)}, ...), condition=%wide.region_27.29_spmd.clone, body=%wide.region_22.28_spmd.clone.sunk | while | flops 2724331520 | bytes 161284432 | solution.py:247
  978.3 8.5 bitcast_convert_fusion
  988.8 9.6 fusion.159
  1000.2 9.5 fusion.158
  1011.1 4.8 fusion.157
  1015.9 3.8 copy.157
  1020.3 11.6 reduce.24
  1031.8 4.7 reshape.367
  1036.5 5.7 all-to-all-start
  1042.3 8.7 fusion.138
  1057.3 11.6 reduce.23
  1068.9 4.6 reshape.369
  1073.5 9.1 all-to-all-done
  1082.6 19.2 %all-to-all-start.2 = ((bf16[16,2,24576]{2,1,0:T(2,128)(2,1)}), bf16[16,2,24576]{2,1,0:T(2,128)(2,1)}, u32[]{:S(2)}, u32[]{:S(2)}) async-start(bf16[16,2,24576]{2,1,0:T(2,128)(2,1)} %reshape.369), calls=%async_computation.6 | async-start | bytes 3145728 | tf_op jit(solution)/shard_map/all_to_all | solution.py:306
  1102.0 10.1 reshape.368
  1112.1 3.4 copy.152
  1115.5 3.3 gather_fusion.2
  1119.9 48.6 %all-reduce = (f32[2,768]{1,0:T(2,128)S(1)}, f32[6,768]{1,0:T(8,128)S(1)}, f32[3072]{0:T(1024)S(1)}) all-reduce(f32[2,768]{1,0:T(2,128)S(1)} %constant_dynamic-update-slice_fusion, f32[6,768]{1,0:T(8,128)S(1)} %stack.108, f32[3072]{0:T(1024)S(1)} %dynamic_update_slice.24), channel_id=1, replica_groups=mesh['dp'=16,'tensor'=2] {'dp','tensor'}, use_global_device_ids=true, to_apply=%region_35.37 | all-reduce | flops 9216 | bytes 73728 | tf_op jit(solution)/shard_map/psum | solution.py:299
  1170.4 8.1 reshape.370
  1179.9 3.3 gather_fusion.4
  1183.2 3.4 fusion.145
  1186.6 28.2 %reduce-scatter.21.cloned.1.call-done = f32[48,1536]{1,0:T(8,128)} async-done(((f32[768,1536]{1,0:T(8,128)}), f32[48,1536]{1,0:T(8,128)}) %reduce-scatter.21.cloned.1.call-update) | async-done | bytes 294928 | tf_op jit(solution)/shard_map/reduce_scatter | solution.py:284
  1214.8 61.4 %reduce-scatter.19.cloned.1.call-done = f32[48,384]{1,0:T(8,128)} async-done(((f32[768,384]{1,0:T(8,128)}), f32[48,384]{1,0:T(8,128)}) %reduce-scatter.19.cloned.1.call-update) | async-done | bytes 73744 | tf_op jit(solution)/shard_map/reduce_scatter | solution.py:283
  1276.2 71.6 %reduce-scatter.17.cloned.1.call-done = f32[48,3,384]{2,0,1:T(8,128)} async-done(((f32[768,3,384]{2,0,1:T(8,128)}), f32[48,3,384]{2,0,1:T(8,128)}) %reduce-scatter.17.cloned.1.call-update) | async-done | bytes 221200 | tf_op jit(solution)/shard_map/reduce_scatter | solution.py:282
  (543 shorter events, 399.0 us)
Async XLA Ops:
  7.2 126.4 %all-gather.8.cloned.1.call-start = ((), (), s32[]{:S(2)}) async-start(), calls=%async_computation.11 | async-start | bytes 4718592 | tf_op jit(solution)/shard_map/all_gather | solution.py:174
  8.1 8.0 copy-start.43
  10.7 71.8 %collective-permute-start.14 = (bf16[1,1,64,768]{3,2,0,1:T(8,128)(2,1)S(1)}, bf16[1,1,64,768]{3,2,0,1:T(8,128)(2,1)S(1)}, u32[]{:S(2)}, u32[]{:S(2)}) collective-permute-start(bf16[1,1,64,768]{3,2,0,1:T(8,128)(2,1)S(1)} %constant_dynamic-slice_fusion.2), channel_id=1, source_target_pairs={{0,30},{2,0},{4,2},{6,4},{8,6},{10,8},{12,10},{14,12},{16,14},{18,... | collective-permute-start | bytes 294920 | tf_op jit(solution)/shard_map/ppermute | solution.py:31
  16.6 65.8 %collective-permute-start.13 = (bf16[1,1,64,768]{3,2,1,0:T(8,128)(2,1)S(1)}, bf16[1,1,64,768]{3,2,1,0:T(8,128)(2,1)S(1)}, u32[]{:S(2)}, u32[]{:S(2)}) collective-permute-start(bf16[1,1,64,768]{3,2,1,0:T(8,128)(2,1)S(1)} %get-tuple-element.269), channel_id=1, source_target_pairs={{0,28},{2,30},{4,0},{6,2},{8,4},{10,6},{12,8},{14,10},{16,12},{18,... | collective-permute-start | bytes 294920 | tf_op jit(solution)/shard_map/ppermute | solution.py:31
  17.4 65.0 %collective-permute-start.12 = (bf16[1,1,64,768]{3,2,1,0:T(8,128)(2,1)S(1)}, bf16[1,1,64,768]{3,2,1,0:T(8,128)(2,1)S(1)}, u32[]{:S(2)}, u32[]{:S(2)}) collective-permute-start(bf16[1,1,64,768]{3,2,1,0:T(8,128)(2,1)S(1)} %get-tuple-element.270), channel_id=1, source_target_pairs={{0,26},{2,28},{4,30},{6,0},{8,2},{10,4},{12,6},{14,8},{16,10},{18,... | collective-permute-start | bytes 294920 | tf_op jit(solution)/shard_map/ppermute | solution.py:31
  17.5 64.8 %collective-permute-start.11 = (bf16[1,1,64,768]{3,2,1,0:T(8,128)(2,1)S(1)}, bf16[1,1,64,768]{3,2,1,0:T(8,128)(2,1)S(1)}, u32[]{:S(2)}, u32[]{:S(2)}) collective-permute-start(bf16[1,1,64,768]{3,2,1,0:T(8,128)(2,1)S(1)} %get-tuple-element.271), channel_id=1, source_target_pairs={{0,24},{2,26},{4,28},{6,30},{8,0},{10,2},{12,4},{14,6},{16,8},{18,... | collective-permute-start | bytes 294920 | tf_op jit(solution)/shard_map/ppermute | solution.py:31
  17.9 6.9 collective-permute-start
  24.8 7.3 collective-permute-start.1
  32.2 5.8 collective-permute-start.2
  38.0 6.4 collective-permute-start.3
  44.4 5.8 collective-permute-start.4
  50.3 6.4 collective-permute-start.5
  56.7 5.6 collective-permute-start.6
  62.3 5.5 collective-permute-start.7
  67.8 16.5 %copy-start.29 = (f32[48,3,384]{2,0,1:T(8,128)S(1)}, f32[48,3,384]{2,0,1:T(8,128)}, u32[]{:S(2)}) copy-start(f32[48,3,384]{2,0,1:T(8,128)} %param.26) | copy-start | bytes 663556
  67.8 4.9 collective-permute-start.8
  72.8 5.5 collective-permute-start.9
  78.3 6.8 copy-start.52
  78.3 7.4 copy-start.47
  78.3 7.6 copy-start.31
  78.3 4.0 collective-permute-start.10
  84.3 92.7 %all-gather.10.cloned.1.call-start = ((), (), s32[]{:S(2)}) async-start(), calls=%async_computation.12 | async-start | bytes 1880064 | tf_op jit(solution)/shard_map/all_gather | solution.py:162
  85.0 292.8 %reduce-scatter.9.cloned.1.call-start = ((), (), s32[]{:S(2)}) async-start(), calls=%async_computation.13 | async-start | bytes 4718592 | tf_op jit(solution)/shard_map/reduce_scatter | solution.py:188
  329.4 6.2 copy-start.2
  335.5 42.3 %copy-start.30 = (f32[768]{0:T(1024)S(1)}, f32[768]{0:T(1024)}, u32[]{:S(2)}) copy-start(f32[768]{0:T(1024)} %param.31) | copy-start | bytes 9220
  335.5 42.3 %copy-start.4 = (bf16[16,64,768]{2,1,0:T(8,128)(2,1)S(1)}, bf16[16,64,768]{2,1,0:T(8,128)(2,1)}, u32[]{:S(2)}) copy-start(bf16[16,64,768]{2,1,0:T(8,128)(2,1)} %gather_fusion) | copy-start | bytes 4718596
  335.6 87.3 %all-gather.14.cloned.1.call-start = ((), (), s32[]{:S(2)}) async-start(), calls=%async_computation.15 | async-start | bytes 2506752 | tf_op jit(solution)/shard_map/all_gather | solution.py:164
  337.2 43.7 %copy-start.32 = (f32[768]{0:T(1024)S(1)}, f32[768]{0:T(1024)}, u32[]{:S(2)}) copy-start(f32[768]{0:T(1024)} %param.34) | copy-start | bytes 9220
  337.2 43.7 %copy-start.39 = (f32[768]{0:T(1024)S(1)}, f32[768]{0:T(1024)}, u32[]{:S(2)}) copy-start(f32[768]{0:T(1024)} %param.35) | copy-start | bytes 9220
  337.2 131.3 %all-gather.12.cloned.1.call-start = ((), (), s32[]{:S(2)}) async-start(), calls=%async_computation.14 | async-start | bytes 4718592 | tf_op jit(solution)/shard_map/all_gather | solution.py:199
  380.9 87.6 %copy-start.51 = (f32[1536]{0:T(1024)S(1)}, f32[1536]{0:T(1024)}, u32[]{:S(2)}) copy-start(f32[1536]{0:T(1024)} %param.32) | copy-start | bytes 18436
  383.0 130.6 %all-gather.16.cloned.1.call-start = ((), (), s32[]{:S(2)}) async-start(), calls=%async_computation.16 | async-start | bytes 2506752 | tf_op jit(solution)/shard_map/all_gather | solution.py:165
  383.7 186.1 %reduce-scatter.11.cloned.1.call-start = ((), (), s32[]{:S(2)}) async-start(), calls=%async_computation.17 | async-start | bytes 4718592 | tf_op jit(solution)/shard_map/reduce_scatter | solution.py:202
  522.7 102.1 %all-gather.18.cloned.1.call-start = ((), (), s32[]{:S(2)}) async-start(), calls=%async_computation.18 | async-start | bytes 4718592 | tf_op jit(solution)/shard_map/all_gather | solution.py:223
  526.0 42.4 %copy-start.33 = (f32[768]{0:T(1024)S(1)}, f32[768]{0:T(1024)}, u32[]{:S(2)}) copy-start(f32[768]{0:T(1024)} %param.36) | copy-start | bytes 9220
  527.7 42.1 %copy-start.45 = (f32[768]{0:T(1024)S(1)}, f32[768]{0:T(1024)}, u32[]{:S(2)}) copy-start(f32[768]{0:T(1024)} %param.33) | copy-start | bytes 9220
  579.3 110.6 %reduce-scatter.13.cloned.1.call-start = ((), (), s32[]{:S(2)}) async-start(), calls=%async_computation.19 | async-start | bytes 4718592 | tf_op jit(solution)/shard_map/reduce_scatter | solution.py:230
  624.7 15.1 %copy-start.50 = (bf16[768,1536]{1,0:T(8,128)(2,1)S(1)}, bf16[768,1536]{1,0:T(8,128)(2,1)}, u32[]{:S(2)}) copy-start(bf16[768,1536]{1,0:T(8,128)(2,1)} %all-gather.14.cloned.1.call-done) | copy-start | bytes 7077892
  646.2 98.7 %all-gather.20.cloned.1.call-start = ((), (), s32[]{:S(2)}) async-start(), calls=%async_computation.20 | async-start | bytes 4718592 | tf_op jit(solution)/shard_map/all_gather | solution.py:242
  689.8 4.6 copy-start.10
  689.8 4.6 copy-start.20
  698.5 46.4 %copy-start.26 = (bf16[768,384]{1,0:T(8,128)(2,1)S(1)}, bf16[768,384]{1,0:T(8,128)(2,1)}, u32[]{:S(2)}) copy-start(bf16[768,384]{1,0:T(8,128)(2,1)} %all_gather.30) | copy-start | bytes 1769476
  699.8 351.2 %reduce-scatter.15.cloned.1.call-start = ((), (), s32[]{:S(2)}) async-start(), calls=%async_computation.21 | async-start | bytes 4718592 | tf_op jit(solution)/shard_map/reduce_scatter | solution.py:273
  751.1 4.0 copy-start.3
  972.4 4.4 copy-start.13
  986.9 199.7 %reduce-scatter.23.cloned.1.call-start = ((), (), s32[]{:S(2)}) async-start(), calls=%async_computation.25 | async-start | bytes 5013504 | tf_op jit(solution)/shard_map/reduce_scatter | solution.py:285
  998.4 216.5 %reduce-scatter.21.cloned.1.call-start = ((), (), s32[]{:S(2)}) async-start(), calls=%async_computation.24 | async-start | bytes 5013504 | tf_op jit(solution)/shard_map/reduce_scatter | solution.py:284
  1009.7 266.5 %reduce-scatter.19.cloned.1.call-start = ((), (), s32[]{:S(2)}) async-start(), calls=%async_computation.23 | async-start | bytes 1253376 | tf_op jit(solution)/shard_map/reduce_scatter | solution.py:283
  1031.8 10.4 copy-start.23
  1031.8 10.4 copy-start.24
  1036.5 46.1 %all-to-all-start = ((bf16[16,2,24576]{2,1,0:T(2,128)(2,1)}), bf16[16,2,24576]{2,1,0:T(2,128)(2,1)}, u32[]{:S(2)}, u32[]{:S(2)}) async-start(bf16[16,2,24576]{2,1,0:T(2,128)(2,1)} %reshape.367), calls=%async_computation.2 | async-start | bytes 3145728 | tf_op jit(solution)/shard_map/all_to_all | solution.py:303
  1042.2 305.6 %reduce-scatter.17.cloned.1.call-start = ((), (), s32[]{:S(2)}) async-start(), calls=%async_computation.22 | async-start | bytes 3760128 | tf_op jit(solution)/shard_map/reduce_scatter | solution.py:282
  1068.9 33.0 %copy-start.53 = (s32[16]{0:T(128)S(1)}, s32[16]{0:T(128)}, u32[]{:S(2)}) copy-start(s32[16]{0:T(128)} %param.25) | copy-start | bytes 196
  1068.9 33.0 %copy-start.37 = (f32[768]{0:T(1024)S(1)}, f32[768]{0:T(1024)}, u32[]{:S(2)}) copy-start(f32[768]{0:T(1024)} %get-tuple-element.194) | copy-start | bytes 9220
  1068.9 33.0 %copy-start.40 = (f32[768]{0:T(1024)S(1)}, f32[768]{0:T(1024)}, u32[]{:S(2)}) copy-start(f32[768]{0:T(1024)} %get-tuple-element.189) | copy-start | bytes 9220
  1082.6 87.7 %all-to-all-start.2 = ((bf16[16,2,24576]{2,1,0:T(2,128)(2,1)}), bf16[16,2,24576]{2,1,0:T(2,128)(2,1)}, u32[]{:S(2)}, u32[]{:S(2)}) async-start(bf16[16,2,24576]{2,1,0:T(2,128)(2,1)} %reshape.369), calls=%async_computation.6 | async-start | bytes 3145728 | tf_op jit(solution)/shard_map/all_to_all | solution.py:306
  1112.0 6.8 copy-start.41
  1112.0 7.1 copy-start.36
  1112.0 7.1 copy-start.35
  1112.0 7.1 copy-start.34
  1112.1 7.1 copy-start.38
  1112.1 7.2 copy-start.16
  1115.5 4.0 copy-start.14
  1179.9 167.9 %copy-start.1 = (bf16[16,1,64,768]{3,2,1,0:T(8,128)(2,1)S(1)}, bf16[16,1,64,768]{3,2,1,0:T(8,128)(2,1)}, u32[]{:S(2)}) copy-start(bf16[16,1,64,768]{3,2,1,0:T(8,128)(2,1)} %param.22) | copy-start | bytes 4718596
  (43 other events, 101.1 us)
Sparse Core Ops, SparseCore 0:
  84.4 49.1 all-gather.7
  136.5 40.4 all-gather.9
  335.7 42.1 reduce-scatter.8
  380.6 42.2 all-gather.13
  424.9 43.6 all-gather.11
  471.2 42.2 all-gather.15
  522.8 42.1 reduce-scatter.10
  579.4 45.2 all-gather.17
  646.4 43.4 reduce-scatter.12
  700.0 44.8 all-gather.19
  987.0 43.4 reduce-scatter.14
  1034.8 94.6 reduce-scatter.22
  1134.0 80.8 reduce-scatter.20
  1218.9 57.2 reduce-scatter.18
  1280.5 67.2 reduce-scatter.16
